TPU v7x, 32 devices: a whole 2x2x4 slice. The times are simulated.
32 devices in a mesh: rep: 2 (over x), shard: 16 (over z, y, core).
Axes of the slice: x: 2, y: 2, z: 4, core: 2. Of those that a mesh axis runs over, the one named last changes fastest.
Arguments:
- hidden: bfloat16 [12288, 64], P(('rep', 'shard')), may hold values from -6 to 6
- grad_out: bfloat16 [12288, 4096], P(('rep', 'shard')), may hold values from -6 to 6
- weight_band: bfloat16 [64, 4096], P('shard'), may hold values from -0.09375 to 0.09375
- error_feedback: float32 [2, 64, 4096], P('rep', 'shard'), may hold values from -4.2426405 to 4.2426405
- q_start: float32 [4096, 32], replicated, may hold values from -6 to 6
Outputs:
- update: float32 [64, 4096], P('shard')
- error_next: float32 [2, 64, 4096], P('rep', 'shard')
- q_next: float32 [4096, 32], replicated
- d_hidden: bfloat16 [12288, 64], P(('rep', 'shard'))
All inputs are finite; a program needn't handle non-finite values.
Results may differ from a plain program's by a relative error of at most 0.0004.
Values may be sent and summed in bfloat16 or wider, within the bound.
A program may use at most 64 MiB of HBM per device.

v0:
```python
import math

import jax
import jax.numpy as jnp
from jax import lax
from jax.sharding import PartitionSpec as P

POWER = 2


def orthonormal(matrix):
    gram_matrix = jnp.dot(matrix.T, matrix, precision=lax.Precision.HIGHEST)
    factor_low = jnp.linalg.cholesky(gram_matrix)
    return lax.linalg.triangular_solve(
        factor_low, matrix, left_side=False, lower=True, transpose_a=True
    )


def orth_rows(p_local):
    all_rows = lax.all_gather(p_local, "shard", axis=0, tiled=True)
    gram_matrix = jnp.dot(all_rows.T, all_rows, precision=lax.Precision.HIGHEST)
    factor_low = jnp.linalg.cholesky(gram_matrix)
    return lax.linalg.triangular_solve(
        factor_low, p_local, left_side=False, lower=True, transpose_a=True
    )


def body(hidden, grad_out, weight_band, error_feedback, q_start):
    n_rep = lax.axis_size("rep")
    n_shard = lax.axis_size("shard")
    token_rows = hidden.shape[0]
    grad_scale = 1.0 / math.sqrt(token_rows * n_shard * n_rep)
    d_hidden = lax.dot_general(
        grad_out,
        lax.all_gather(weight_band, "shard", axis=0, tiled=True),
        (((1,), (1,)), ((), ())),
        preferred_element_type=jnp.float32,
    ).astype(jnp.bfloat16)
    grad_rows = lax.psum_scatter(
        lax.dot_general(
            hidden, grad_out, (((0,), (0,)), ((), ())), preferred_element_type=jnp.float32
        )
        * grad_scale,
        "shard",
        scatter_dimension=0,
        tiled=True,
    )
    own_rows = grad_rows + error_feedback[0]
    q_factor = q_start
    p_factor = None
    for round_index in range(POWER):
        q_hat = orthonormal(q_factor)
        p_local = jnp.dot(own_rows, q_hat, precision=lax.Precision.HIGHEST)
        p_factor = orth_rows(lax.psum(p_local, "rep"))
        q_term = lax.dot_general(
            own_rows, p_factor, (((0,), (0,)), ((), ())), precision=lax.Precision.HIGHEST
        )
        q_factor = lax.psum(q_term, ("rep", "shard"))
    update = jnp.dot(p_factor, q_factor.T, precision=lax.Precision.HIGHEST)
    error_next = own_rows - update / n_rep
    return (update, error_next[None], q_factor, d_hidden)


def solution(mesh):
    return jax.shard_map(
        body,
        mesh=mesh,
        in_specs=(
            P(("rep", "shard"), None),
            P(("rep", "shard"), None),
            P("shard", None),
            P("rep", "shard", None),
            P(),
        ),
        out_specs=(P("shard", None), P("rep", "shard", None), P(), P(("rep", "shard"), None)),
        check_vma=False,
    )
```

profile of v0, /device:TPU:9, one launch (start us, length us, event | category | flops | bytes accessed | tf_op | source)
XLA Modules:
  0.0 447.9 jit_solution(12840853244050156011)
XLA Ops:
  7.2 1.8 copy-done
  9.1 2.5 convolution_multiply_fusion
  11.6 1.8 fusion.18
  13.5 2.9 cholesky.74
  17.1 0.7 fusion
  17.8 2.4 custom-call.10
  21.5 2.5 convolution_bitcast_fusion.1
  23.9 81.3 %all-reduce.9.cloned.1.call-done = f32[64,4096]{1,0:T(8,128)} async-done(((f32[64,4096]{1,0:T(8,128)}), f32[64,4096]{1,0:T(8,128)}) %all-reduce.9.cloned.1.call-update) | async-done | bytes 1048592
  105.2 0.9 dynamic-slice_add_fusion
  106.2 1.6 fusion.19
  107.7 3.8 psum.28
  111.5 19.9 %all-gather = f32[16,4,32]{2,1,0:T(4,128)S(1)} all-gather(f32[1,4,32]{2,1,0:T(4,128)S(1)} %bitcast.83), channel_id=1, replica_groups=mesh['rep'=2,'shard'=16] {'shard'}, dimensions={0}, use_global_device_ids=true | all-gather | bytes 8704 | tf_op jit(solution)/shard_map/all_gather | solution.py:20
  131.7 2.9 cholesky.85
  136.0 2.4 custom-call.11
  138.7 1.3 fusion.21
  140.1 20.4 %all-gather.2 = bf16[16,4,4096]{2,1,0:T(4,128)(2,1)} all-gather(bf16[1,4,4096]{2,1,0:T(4,128)(2,1)S(1)} %bitcast.82), channel_id=1, replica_groups=mesh['rep'=2,'shard'=16] {'shard'}, dimensions={0}, use_global_device_ids=true | all-gather | bytes 557056 | tf_op jit(solution)/shard_map/all_gather | solution.py:35
  160.5 2.0 reshape.34
  162.5 104.6 %all-reduce.5.cloned.1.call-done = f32[4096,32]{0,1:T(8,128)} async-done(((f32[4096,32]{0,1:T(8,128)}), f32[4096,32]{0,1:T(8,128)}) %all-reduce.5.cloned.1.call-update) | async-done | bytes 524304 | tf_op jit(solution)/shard_map/psum | solution.py:58
  267.1 1.8 fusion.22
  269.0 2.9 cholesky.96
  273.2 2.4 custom-call.12
  275.7 1.7 convolution_bitcast_fusion
  277.9 3.8 psum.30
  281.6 21.3 %all-gather.1 = f32[16,4,32]{2,1,0:T(4,128)S(1)} all-gather(f32[1,4,32]{2,1,0:T(4,128)S(1)} %bitcast.84), channel_id=1, replica_groups=mesh['rep'=2,'shard'=16] {'shard'}, dimensions={0}, use_global_device_ids=true | all-gather | bytes 8704 | tf_op jit(solution)/shard_map/all_gather | solution.py:20
  303.3 2.9 cholesky.107
  307.5 2.4 custom-call.13
  310.1 1.4 fusion.25
  311.6 2.7 convolution_convert_fusion
  314.3 123.1 %all-reduce.7.cloned.1.call-done = f32[4096,32]{0,1:T(8,128)} async-done(((f32[4096,32]{0,1:T(8,128)}), f32[4096,32]{0,1:T(8,128)}) %all-reduce.7.cloned.1.call-update) | async-done | bytes 524304 | tf_op jit(solution)/shard_map/psum | solution.py:58
  437.4 1.4 fusion.26
  438.8 0.7 subtract_bitcast_fusion
  439.5 1.9 copy.20
  (40 shorter events, 7.1 us)
Async XLA Ops:
  7.2 1.9 copy-start
  7.2 13.0 %copy-start.4 = (u32[32]{0:T(128)S(1)}, u32[32]{0:T(128)}, u32[]{:S(2)}) copy-start(u32[32]{0:T(128)} %constant.41) | copy-start | bytes 388
  7.2 98.0 %copy-start.2 = (f32[1,4,4096]{2,1,0:T(4,128)S(1)}, f32[1,4,4096]{2,1,0:T(4,128)}, u32[]{:S(2)}) copy-start(f32[1,4,4096]{2,1,0:T(4,128)} %param.13) | copy-start | bytes 196612
  7.2 98.0 %all-reduce.9.cloned.1.call-start = ((), (), s32[]{:S(2)}) async-start(), calls=%async_computation.2 | async-start | bytes 2097152
  11.6 128.5 %copy-start.3 = (bf16[4,4096]{1,0:T(4,128)(2,1)S(1)}, bf16[4,4096]{1,0:T(4,128)(2,1)}, u32[]{:S(2)}) copy-start(bf16[4,4096]{1,0:T(4,128)(2,1)} %param.12) | copy-start | bytes 98308
  11.6 255.5 %all-reduce.5.cloned.1.call-start = ((), (), s32[]{:S(2)}) async-start(), calls=%async_computation | async-start | bytes 1048576 | tf_op jit(solution)/shard_map/psum | solution.py:58
  140.0 297.4 %all-reduce.7.cloned.1.call-start = ((), (), s32[]{:S(2)}) async-start(), calls=%async_computation.1 | async-start | bytes 1048576 | tf_op jit(solution)/shard_map/psum | solution.py:58
  438.8 2.5 copy-start.1
Sparse Core Ops, SparseCore 0:
  11.7 93.4 all-reduce.8
  140.1 126.9 all-reduce.4
  311.7 125.6 all-reduce.6
where the time goes:
time: 452 us; the launch traced here: 448 us
  waiting for transfers between devices  309 us (68%)
  blocking collectives  69.2 us (15%)
  other arithmetic  28.3 us (6%)
  matrix products  20 us (4%)
  between operations  14.6 us (3%)
  local copies, waits for them, and re-layouts  6.59 us (1%)
    psum x2, waiting for transfers between devices, body(): q_factor = lax.psum(q_term, ('rep', 'shard'))  228 us
    unnamed x4, waiting for transfers between devices  81.3 us
    all_gather x2, blocking collectives, orth_rows(): all_rows = lax.all_gather(p_local, 'shard', axis=0, tiled=True)  41.2 us
    all_gather x1, blocking collectives, body(): lax.all_gather(weight_band, 'shard', axis=0, tiled=True)  20.4 us
  transfers between devices with their start and end apart: 3, of which 3 were waited for; matrix products, arithmetic and copies ran while one was open for 4% of the time, Pallas kernels for 0%

commit v1 on v0

v1 whole, which is shorter than its diff:
```python
import functools
import math

import jax
import jax.numpy as jnp
from jax import lax
from jax.experimental import pallas as pl
from jax.experimental.pallas import tpu as pltpu
from jax.sharding import PartitionSpec as P

HIGHEST = lax.Precision.HIGHEST
NT = (((1,), (1,)), ((), ()))
NN = (((1,), (0,)), ((), ()))


def dot32(a, b, dims):
    return lax.dot_general(a, b, dims, precision=HIGHEST, preferred_element_type=jnp.float32)


def orth_rows(v):
    rank = v.shape[0]
    v = v * (1.0 / jnp.max(jnp.abs(v), axis=1, keepdims=True))
    rows = lax.broadcasted_iota(jnp.int32, (rank, 1), 0)
    for j in range(rank):
        pivot = v[j : j + 1, :]
        dots = jnp.sum(v * pivot, axis=1, keepdims=True)
        coef = jnp.where(rows > j, dots * (1.0 / dots[j : j + 1, :]), 0.0)
        v = v - coef * pivot
    return v * lax.rsqrt(jnp.sum(v * v, axis=1, keepdims=True))


def kernel(
    n_rep, n_shard, power, scale,
    h_ref, g_hbm, w_ref, ef_ref, q0_hbm,
    upd_ref, err_ref, qn_ref, dh_ref,
    gbuf, q0buf, part, oth, sib, rs, rep, mrow_s, mrow_r, wst, wsib, wa, qall, wall, wf,
    g_sem, q0_sem, d2d_s, d2d_r, rs_s, rs_r, rep_s, rep_r, mr_s, mr_r, ws_s, ws_r, wa_s, wa_r,
    q_s, q_r, qf_s, w_s, w_r, wfw_s,
):
    me = lax.axis_index("shard")
    my_rep = lax.axis_index("rep")
    n_chip = n_shard // 2
    chip = me // 2
    core = me % 2
    mate = chip * 2 + (1 - core)
    bucket = h_ref.shape[0]
    cols = rs.shape[2]
    own = ef_ref.shape[0]
    even = core == 0

    def chip_at(k):
        return lax.rem(chip + k, n_chip)

    def wide(c):
        return pl.ds(pl.multiple_of(c * (2 * cols), 2 * cols), 2 * cols)

    def remote(src, dst, ssem, rsem, **where):
        return pltpu.make_async_remote_copy(
            src_ref=src, dst_ref=dst, send_sem=ssem, recv_sem=rsem,
            device_id=where, device_id_type=pl.DeviceIdType.MESH,
        )

    order = list(range(n_chip - 1, 0, -1)) + [0]

    barrier = pltpu.get_barrier_semaphore()
    for k in range(1, n_shard):
        pl.semaphore_signal(
            barrier, inc=1, device_id={"shard": lax.rem(me + k, n_shard)},
            device_id_type=pl.DeviceIdType.MESH,
        )
    for k in range(1, n_rep):
        pl.semaphore_signal(
            barrier, inc=1, device_id={"rep": lax.rem(my_rep + k, n_rep)},
            device_id_type=pl.DeviceIdType.MESH,
        )

    def load(k):
        return pltpu.make_async_copy(g_hbm.at[:, wide(chip_at(k))], gbuf.at[k], g_sem.at[k])

    for k in order:
        load(k).start()
    q0_load = pltpu.make_async_copy(q0_hbm.at[:, wide(chip)], q0buf, q0_sem)
    q0_load.start()

    own_row = lax.broadcasted_iota(jnp.int32, (bucket, 1), 0) // own == me
    hidden = h_ref[...]

    def pair(k):
        return remote(oth.at[k], sib.at[k], d2d_s.at[k], d2d_r.at[k], shard=mate)

    for at, k in enumerate(order):
        load(k).wait()
        block = lax.dot_general(
            hidden, gbuf[k], NN, preferred_element_type=jnp.float32
        ) * scale
        error = jnp.concatenate([ef_ref[:, wide(chip_at(k))]] * n_shard, axis=0)
        block = block + jnp.where(own_row, error, 0.0)
        low, high = block[:, :cols], block[:, cols:]
        oth[k] = jnp.where(even, high, low)
        part[k] = jnp.where(even, low, high)
        if at == 0:
            pl.semaphore_wait(barrier, n_shard - 1 + n_rep - 1)
        pair(k).start()

    def scatter(k):
        return remote(
            part.at[k], rs.at[k], rs_s.at[k], rs_r.at[k], shard=chip_at(k) * 2 + core
        )

    for k in order:
        pair(k).wait_recv()
        part[k] = part[k] + sib[k]
        if k:
            scatter(k).start()
    merged = part[0]
    for k in order[:-1]:
        scatter(k).wait_recv()
        merged = merged + rs[k]
    rep[my_rep] = merged

    def across(k):
        other = lax.rem(my_rep + k, n_rep)
        return remote(
            rep.at[my_rep], rep.at[my_rep], rep_s.at[k], rep_r.at[k], rep=other
        )

    for k in range(1, n_rep):
        across(k).start()
    for s in range(n_shard):
        mrow_s[s] = merged[s * own : (s + 1) * own, :]
    mrow_r[me] = mrow_s[me]

    def row_send(k):
        to = lax.rem(me + k, n_shard)
        return remote(mrow_s.at[to], mrow_r.at[me], mr_s.at[k], mr_r.at[k], shard=to)

    for k in range(1, n_shard):
        row_send(k).start()
    for k in range(1, n_rep):
        across(k).wait_recv()
    summed = rep[0]
    for r in range(1, n_rep):
        summed = summed + rep[r]

    q0_load.wait()
    q_own = jnp.where(even, q0buf[:, :cols], q0buf[:, cols:])
    rank = q_own.shape[0]
    half = (bucket + rank) // 2
    term = dot32(jnp.concatenate([summed, q_own], axis=0), summed, NT)
    wst[...] = jnp.concatenate([term[:half], term[half:]], axis=1)
    mate_copy = remote(wst, wsib, ws_s.at[0], ws_r.at[0], shard=mate)
    mate_copy.start()
    mate_copy.wait_recv()
    wa[chip] = wst[...] + wsib[...]

    def term_send(k):
        return remote(
            wa.at[chip], wa.at[chip], wa_s.at[k], wa_r.at[k], shard=chip_at(k) * 2 + core
        )

    for k in order[:-1]:
        term_send(k).start()

    def w_send(k):
        to = mate if k == 0 else chip_at(k) * 2 + core
        return remote(w_ref, wall.at[me], w_s.at[k], w_r.at[k], shard=to)

    for k in order:
        w_send(k).start()
    wall[me] = w_ref[...]

    for k in order[:-1]:
        term_send(k).wait_recv()
    total = wa[0]
    for c in range(1, n_chip):
        total = total + wa[c]
    total = jnp.concatenate([total[:, :bucket], total[:, bucket:]], axis=0)
    square, y = total[:bucket], total[bucket:]
    p = orth_rows(y)
    for _ in range(power - 1):
        p = orth_rows(dot32(p, square, NN))

    qall[me] = dot32(p, summed, NN)

    def q_send(k):
        to = mate if k == 0 else chip_at(k) * 2 + core
        return remote(qall.at[me], qall.at[me], q_s.at[k], q_r.at[k], shard=to)

    for k in order:
        q_send(k).start()

    def source(k):
        return lax.rem(chip + n_chip - k, n_chip) * 2

    def w_pass(k):
        at = source(k) + core
        return remote(wall.at[at], wall.at[at], wfw_s.at[k], w_r.at[n_chip + k], shard=mate)

    def q_pass(k):
        at = source(k) + core
        return remote(qall.at[at], qall.at[at], qf_s.at[k], q_r.at[n_chip + k], shard=mate)

    for k in order[:-1]:
        w_send(k).wait_recv()
        w_pass(k).start()
    w_send(0).wait_recv()
    for k in order[:-1]:
        w_pass(k).wait_recv()
    for s in range(n_shard):
        wf[s * own : (s + 1) * own, :] = wall[s].astype(jnp.float32)
    dh = jnp.zeros(dh_ref.shape, jnp.float32)
    for k in range(n_chip):
        band = wf[:, wide(chip_at(k))].astype(jnp.bfloat16)
        dh = dh + lax.dot_general(band, gbuf[k], NT, preferred_element_type=jnp.float32)
    dh_ref[...] = dh.astype(jnp.bfloat16)

    for k in order[:-1]:
        q_send(k).wait_recv()
        q_pass(k).start()
    q_send(0).wait_recv()
    for k in order[:-1]:
        q_pass(k).wait_recv()
    for k in range(1, n_shard):
        row_send(k).wait_recv()

    pick = lax.broadcasted_iota(jnp.int32, (8, bucket), 1) == me * own + lax.broadcasted_iota(
        jnp.int32, (8, bucket), 0
    )
    p_own = dot32(pick.astype(jnp.float32), p, NT)
    for s in range(n_shard):
        here = slice(s * cols, (s + 1) * cols)
        q = qall[s]
        qn_ref[:, here] = q
        update = dot32(p_own, q, NN)[:own]
        upd_ref[:, here] = update
        err_ref[:, here] = mrow_r[s] - update * (1.0 / n_rep)

    for k in order:
        pair(k).wait_send()
        w_send(k).wait_send()
        q_send(k).wait_send()
        if k:
            scatter(k).wait_send()
            term_send(k).wait_send()
            w_pass(k).wait_send()
            q_pass(k).wait_send()
    mate_copy.wait_send()
    for k in range(1, n_rep):
        across(k).wait_send()
    for k in range(1, n_shard):
        row_send(k).wait_send()


POWER = 2


def body(n_rep, n_shard, hidden, grad_out, weight_band, error_feedback, q_start):
    tokens, bucket = hidden.shape
    width = grad_out.shape[1]
    own = weight_band.shape[0]
    rank = q_start.shape[1]
    cols = width // n_shard
    n_chip = n_shard // 2
    scale = 1.0 / math.sqrt(tokens * n_shard * n_rep)
    f32, bf16 = jnp.float32, jnp.bfloat16
    half = (bucket + rank) // 2
    dma = lambda *s: pltpu.SemaphoreType.DMA(s)
    vmem = pl.BlockSpec(memory_space=pltpu.VMEM)
    hbm = pl.BlockSpec(memory_space=pl.ANY)
    update, error, q_t, dh_t = pl.pallas_call(
        functools.partial(kernel, n_rep, n_shard, POWER, scale),
        out_shape=(
            jax.ShapeDtypeStruct((own, width), f32),
            jax.ShapeDtypeStruct((own, width), f32),
            jax.ShapeDtypeStruct((rank, width), f32),
            jax.ShapeDtypeStruct((bucket, tokens), bf16),
        ),
        in_specs=[vmem, hbm, vmem, vmem, hbm],
        out_specs=(vmem,) * 4,
        scratch_shapes=[
            pltpu.VMEM((n_chip, tokens, 2 * cols), bf16),
            pltpu.VMEM((rank, 2 * cols), f32),
            pltpu.VMEM((n_chip, bucket, cols), f32),
            pltpu.VMEM((n_chip, bucket, cols), f32),
            pltpu.VMEM((n_chip, bucket, cols), f32),
            pltpu.VMEM((n_chip, bucket, cols), f32),
            pltpu.VMEM((n_rep, bucket, cols), f32),
            pltpu.VMEM((n_shard, own, cols), f32),
            pltpu.VMEM((n_shard, own, cols), f32),
            pltpu.VMEM((half, 2 * bucket), f32),
            pltpu.VMEM((half, 2 * bucket), f32),
            pltpu.VMEM((n_chip, half, 2 * bucket), f32),
            pltpu.VMEM((n_shard, rank, cols), f32),
            pltpu.VMEM((n_shard, own, width), bf16),
            pltpu.VMEM((bucket, width), f32),
            dma(n_chip), dma(), dma(n_chip), dma(n_chip), dma(n_chip), dma(n_chip),
            dma(n_rep), dma(n_rep), dma(n_shard), dma(n_shard), dma(1), dma(1),
            dma(n_chip), dma(n_chip),
            dma(n_chip), dma(n_shard), dma(n_chip), dma(n_chip), dma(n_shard), dma(n_chip),
        ],
        compiler_params=pltpu.CompilerParams(
            collective_id=0, has_side_effects=True, vmem_limit_bytes=60 * 1024 * 1024
        ),
        name="bucket_step",
    )(hidden.T, grad_out, weight_band, error_feedback[0], q_start.T)
    return update, error[None], q_t.T, dh_t.T


def solution(mesh):
    return jax.shard_map(
        functools.partial(body, mesh.shape["rep"], mesh.shape["shard"]),
        mesh=mesh,
        in_specs=(
            P(("rep", "shard"), None),
            P(("rep", "shard"), None),
            P("shard", None),
            P("rep", "shard", None),
            P(),
        ),
        out_specs=(P("shard", None), P("rep", "shard", None), P(), P(("rep", "shard"), None)),
        check_vma=False,
    )
```

time: 452 us -> 57.8 us (0.13)
  waiting for transfers between devices: 309 us -> 0 us
  blocking collectives: 69.2 us -> 0 us
  Pallas kernels: 0 us -> 50.5 us
  other arithmetic: 28.3 us -> 0 us
  matrix products: 20 us -> 0 us
  between operations: 14.6 us -> 0.64 us
    psum x2 -> x0, waiting for transfers between devices: 228 us -> none  [body(): q_factor = lax.psum(q_term, ('rep', 'shard'))]
    unnamed x4 -> x0, waiting for transfers between devices: 81.3 us -> none
    all_gather x3 -> x0, blocking collectives: 61.7 us -> none  [the longest x2 41.2 us: orth_rows(): all_rows = lax.all_gather(p_local, 'shard', axis=0, tiled=True)]
    pallas_call x0 -> x1, Pallas kernels: none -> 50.5 us  [body(): pl.pallas_call(functools.partial(kernel, n_rep, n_shard, POWER, scale), o...]
    another operation x20 -> x0, other arithmetic: 26.7 us -> none  [the longest x6 7.2 us: orth_rows(): factor_low = jnp.linalg.cholesky(gram_matrix)]
    dot_general x11 -> x0, matrix products: 15.4 us -> none  [the longest x2 3.52 us: orthonormal(): gram_matrix = jnp.dot(matrix.T, matrix, precision=lax.Precision.HIGHEST)]
    psum x2 -> x0, blocking collectives: 7.54 us -> none  [body(): p_factor = orth_rows(lax.psum(p_local, 'rep'))]
    another operation x4 -> x0, matrix products: 4.55 us -> none  [the longest x2 4.16 us: orthonormal(): lax.linalg.triangular_solve(factor_low, matrix, left_side=False, lower=Tr...]
  transfers between devices with their start and end apart: 3 -> 0, of which waited for: 3 -> 0; matrix products, arithmetic and copies ran while one was open for 4% -> 0% of each run, Pallas kernels for 0% -> 0%
where the time goes in v1:
time: 57.8 us; the launch traced here: 57.4 us
  Pallas kernels  50.5 us (87%)
  local copies, waits for them, and re-layouts  6.24 us (11%)
  between operations  0.64 us (1%)
    pallas_call x1, Pallas kernels, body(): pl.pallas_call(functools.partial(kernel, n_rep, n_shard, POWER, scale), o...  50.5 us
    unnamed x4, local copies, waits for them, and re-layouts  6.24 us

profile of v1, /device:TPU:9, one launch (start us, length us, event | category | flops | bytes accessed | tf_op | source)
XLA Modules:
  0.0 57.4 jit_solution(13361188267098651265)
XLA Ops:
  0.6 50.5 %bucket_step.1 = (f32[4,4096]{1,0:T(4,128)}, f32[4,4096]{1,0:T(4,128)}, f32[32,4096]{1,0:T(8,128)}, bf16[64,384]{1,0:T(8,128)(2,1)}) custom-call(bf16[64,384]{1,0:T(8,128)(2,1)} %bitcast.11, bf16[384,4096]{1,0:T(8,128)(2,1)} %g_hbm.1, bf16[4,4096]{1,0:T(4,128)(2,1)} %w_ref.1, f32[4,4096]{1,0:T(4,128)} %bitcast.9, f32[32,4096]{1,0:T(8,128)} %bitcast.7), custom_call_target="tpu_custom_call" | custom-call | tf_op jit(solution)/shard_map/bucket_step/pallas_call | solution.py:270
  51.2 1.5 %copy.13 = f32[4,4096]{1,0:T(4,128)} copy(f32[4,4096]{1,0:T(4,128)} %get-tuple-element.16) | data formatting | bytes 131072
  52.7 1.5 %copy.14 = f32[1,4,4096]{2,1,0:T(4,128)} copy(f32[1,4,4096]{2,1,0:T(4,128)} %bitcast.8) | data formatting | bytes 131072
  54.1 1.9 %copy.15 = f32[4096,32]{0,1:T(8,128)} copy(f32[4096,32]{0,1:T(8,128)} %bitcast.6) | data formatting | bytes 1048576
  56.0 1.4 %copy.16 = bf16[384,64]{0,1:T(8,128)(2,1)} copy(bf16[384,64]{0,1:T(8,128)(2,1)} %bitcast.10) | data formatting | bytes 98304

commit v2 on v1

--- a/solution.py
+++ b/solution.py
@@ -9,6 +9,9 @@
 from jax.sharding import PartitionSpec as P
 
 HIGHEST = lax.Precision.HIGHEST
+GROUP = 4
+FINISH_LIMIT = 67043328
+VMEM_LIMIT = 67043328
 NT = (((1,), (1,)), ((), ()))
 NN = (((1,), (0,)), ((), ()))
 
@@ -21,21 +24,32 @@
     rank = v.shape[0]
     v = v * (1.0 / jnp.max(jnp.abs(v), axis=1, keepdims=True))
     rows = lax.broadcasted_iota(jnp.int32, (rank, 1), 0)
-    for j in range(rank):
-        pivot = v[j : j + 1, :]
-        dots = jnp.sum(v * pivot, axis=1, keepdims=True)
-        coef = jnp.where(rows > j, dots * (1.0 / dots[j : j + 1, :]), 0.0)
-        v = v - coef * pivot
+    for first in range(0, rank, GROUP):
+        pivots, dots, invs = [], [], []
+        raw = [v[first + i : first + i + 1, :] for i in range(GROUP)]
+        sums = [jnp.sum(v * pivot, axis=1, keepdims=True) for pivot in raw]
+        for i in range(GROUP):
+            at = first + i
+            pivot, dot = raw[i], sums[i]
+            for other, done, inv in zip(pivots, dots, invs):
+                part = done[at : at + 1, :] * inv
+                pivot = pivot - part * other
+                dot = dot - part * done
+            pivots.append(pivot)
+            dots.append(dot)
+            invs.append(1.0 / dot[at : at + 1, :])
+        for i in range(GROUP):
+            v = v - jnp.where(rows > first + i, dots[i] * invs[i], 0.0) * pivots[i]
     return v * lax.rsqrt(jnp.sum(v * v, axis=1, keepdims=True))
 
 
 def kernel(
     n_rep, n_shard, power, scale,
-    h_ref, g_hbm, w_ref, ef_ref, q0_hbm,
-    upd_ref, err_ref, qn_ref, dh_ref,
-    gbuf, q0buf, part, oth, sib, rs, rep, mrow_s, mrow_r, wst, wsib, wa, qall, wall, wf,
+    h_hbm, g_hbm, w_hbm, ef_hbm, q0_hbm,
+    q_out, p_out, row_out, dh_out,
+    h_ref, w_ref, ef_ref, p_ref, dh_ref, gbuf, q0buf, part, oth, sib, rs, rep, mrow_s, mrow_r, wst, wsib, wa, qall, wall, wf,
     g_sem, q0_sem, d2d_s, d2d_r, rs_s, rs_r, rep_s, rep_r, mr_s, mr_r, ws_s, ws_r, wa_s, wa_r,
-    q_s, q_r, qf_s, w_s, w_r, wfw_s,
+    q_s, q_r, qf_s, w_s, w_r, wfw_s, in_sem, out_sem, qo_sem,
 ):
     me = lax.axis_index("shard")
     my_rep = lax.axis_index("rep")
@@ -74,6 +88,13 @@
             device_id_type=pl.DeviceIdType.MESH,
         )
 
+    ins = [
+        pltpu.make_async_copy(src, dst, in_sem.at[i])
+        for i, (src, dst) in enumerate(((h_hbm, h_ref), (ef_hbm, ef_ref), (w_hbm, w_ref)))
+    ]
+    ins[0].start()
+    ins[1].start()
+
     def load(k):
         return pltpu.make_async_copy(g_hbm.at[:, wide(chip_at(k))], gbuf.at[k], g_sem.at[k])
 
@@ -81,9 +102,12 @@
         load(k).start()
     q0_load = pltpu.make_async_copy(q0_hbm.at[:, wide(chip)], q0buf, q0_sem)
     q0_load.start()
+    ins[2].start()
 
     own_row = lax.broadcasted_iota(jnp.int32, (bucket, 1), 0) // own == me
+    ins[0].wait()
     hidden = h_ref[...]
+    ins[1].wait()
 
     def pair(k):
         return remote(oth.at[k], sib.at[k], d2d_s.at[k], d2d_r.at[k], shard=mate)
@@ -165,6 +189,7 @@
         to = mate if k == 0 else chip_at(k) * 2 + core
         return remote(w_ref, wall.at[me], w_s.at[k], w_r.at[k], shard=to)
 
+    ins[2].wait()
     for k in order:
         w_send(k).start()
     wall[me] = w_ref[...]
@@ -214,26 +239,36 @@
         dh = dh + lax.dot_general(band, gbuf[k], NT, preferred_element_type=jnp.float32)
     dh_ref[...] = dh.astype(jnp.bfloat16)
 
-    for k in order[:-1]:
-        q_send(k).wait_recv()
-        q_pass(k).start()
-    q_send(0).wait_recv()
-    for k in order[:-1]:
-        q_pass(k).wait_recv()
-    for k in range(1, n_shard):
-        row_send(k).wait_recv()
-
+    outs = [
+        pltpu.make_async_copy(src, dst, out_sem.at[i])
+        for i, (src, dst) in enumerate(((dh_ref, dh_out), (p_ref, p_out), (mrow_r, row_out)))
+    ]
+    outs[0].start()
     pick = lax.broadcasted_iota(jnp.int32, (8, bucket), 1) == me * own + lax.broadcasted_iota(
         jnp.int32, (8, bucket), 0
     )
-    p_own = dot32(pick.astype(jnp.float32), p, NT)
-    for s in range(n_shard):
-        here = slice(s * cols, (s + 1) * cols)
-        q = qall[s]
-        qn_ref[:, here] = q
-        update = dot32(p_own, q, NN)[:own]
-        upd_ref[:, here] = update
-        err_ref[:, here] = mrow_r[s] - update * (1.0 / n_rep)
+    p_ref[...] = dot32(pick.astype(jnp.float32), p, NT)
+    outs[1].start()
+    for k in range(1, n_shard):
+        row_send(k).wait_recv()
+    outs[2].start()
+
+    def q_write(k, mine):
+        at = source(k) + (core if mine else 1 - core)
+        return pltpu.make_async_copy(
+            qall.at[at], q_out.at[at], qo_sem.at[k if mine else n_chip + k]
+        )
+
+    q_write(0, True).start()
+    for k in order[:-1]:
+        q_send(k).wait_recv()
+        q_pass(k).start()
+        q_write(k, True).start()
+    q_send(0).wait_recv()
+    q_write(0, False).start()
+    for k in order[:-1]:
+        q_pass(k).wait_recv()
+        q_write(k, False).start()
 
     for k in order:
         pair(k).wait_send()
@@ -250,6 +285,45 @@
     for k in range(1, n_shard):
         row_send(k).wait_send()
 
+    for copy in outs:
+        copy.wait()
+    for k in range(n_chip):
+        q_write(k, True).wait()
+        q_write(k, False).wait()
+
+
+def finish(
+    n_rep, n_shard, q_in, p_in, row_in, dh_in,
+    upd_out, err_out, qn_out, dh_out, q_ref, p_ref, row_ref, upd, err, qn, sems, dh_sem, in_sem,
+):
+    own, cols = row_ref.shape[1:]
+    ins = [
+        pltpu.make_async_copy(src, dst, in_sem.at[i])
+        for i, (src, dst) in enumerate(((p_in, p_ref), (row_in, row_ref), (q_in, q_ref)))
+    ]
+    for copy in ins:
+        copy.start()
+    dh_copy = pltpu.make_async_copy(dh_in, dh_out, dh_sem)
+    dh_copy.start()
+    for copy in ins:
+        copy.wait()
+    p_own = p_ref[...]
+    copies = []
+    for c in range(n_shard // 2):
+        here = slice(c * 2 * cols, (c + 1) * 2 * cols)
+        q = jnp.concatenate([q_ref[2 * c], q_ref[2 * c + 1]], axis=1)
+        rows = jnp.concatenate([row_ref[2 * c], row_ref[2 * c + 1]], axis=1)
+        qn[:, here] = q
+        update = dot32(p_own, q, NN)[:own]
+        upd[:, here] = update
+        err[:, here] = rows - update * (1.0 / n_rep)
+        for i, (src, dst) in enumerate(((upd, upd_out), (err, err_out), (qn, qn_out))):
+            copies.append(pltpu.make_async_copy(src.at[:, here], dst.at[:, here], sems.at[i, c]))
+            copies[-1].start()
+    for copy in copies:
+        copy.wait()
+    dh_copy.wait()
+
 
 POWER = 2
 
@@ -265,19 +339,23 @@
     f32, bf16 = jnp.float32, jnp.bfloat16
     half = (bucket + rank) // 2
     dma = lambda *s: pltpu.SemaphoreType.DMA(s)
-    vmem = pl.BlockSpec(memory_space=pltpu.VMEM)
     hbm = pl.BlockSpec(memory_space=pl.ANY)
-    update, error, q_t, dh_t = pl.pallas_call(
+    q3, p_own, rows, dh = pl.pallas_call(
         functools.partial(kernel, n_rep, n_shard, POWER, scale),
         out_shape=(
-            jax.ShapeDtypeStruct((own, width), f32),
-            jax.ShapeDtypeStruct((own, width), f32),
-            jax.ShapeDtypeStruct((rank, width), f32),
+            jax.ShapeDtypeStruct((n_shard, rank, cols), f32),
+            jax.ShapeDtypeStruct((8, rank), f32),
+            jax.ShapeDtypeStruct((n_shard, own, cols), f32),
             jax.ShapeDtypeStruct((bucket, tokens), bf16),
         ),
-        in_specs=[vmem, hbm, vmem, vmem, hbm],
-        out_specs=(vmem,) * 4,
+        in_specs=[pl.BlockSpec(memory_space=pltpu.HBM)] * 5,
+        out_specs=(hbm,) * 4,
         scratch_shapes=[
+            pltpu.VMEM((bucket, tokens), bf16),
+            pltpu.VMEM((own, width), bf16),
+            pltpu.VMEM((own, width), f32),
+            pltpu.VMEM((8, rank), f32),
+            pltpu.VMEM((bucket, tokens), bf16),
             pltpu.VMEM((n_chip, tokens, 2 * cols), bf16),
             pltpu.VMEM((rank, 2 * cols), f32),
             pltpu.VMEM((n_chip, bucket, cols), f32),
@@ -297,12 +375,35 @@
             dma(n_rep), dma(n_rep), dma(n_shard), dma(n_shard), dma(1), dma(1),
             dma(n_chip), dma(n_chip),
             dma(n_chip), dma(n_shard), dma(n_chip), dma(n_chip), dma(n_shard), dma(n_chip),
+            dma(3), dma(3), dma(n_shard),
         ],
         compiler_params=pltpu.CompilerParams(
-            collective_id=0, has_side_effects=True, vmem_limit_bytes=60 * 1024 * 1024
+            collective_id=0, has_side_effects=True, vmem_limit_bytes=VMEM_LIMIT
         ),
         name="bucket_step",
     )(hidden.T, grad_out, weight_band, error_feedback[0], q_start.T)
+    update, error, q_t, dh_t = pl.pallas_call(
+        functools.partial(finish, n_rep, n_shard),
+        out_shape=(
+            jax.ShapeDtypeStruct((own, width), f32),
+            jax.ShapeDtypeStruct((own, width), f32),
+            jax.ShapeDtypeStruct((rank, width), f32),
+            jax.ShapeDtypeStruct((bucket, tokens), bf16),
+        ),
+        in_specs=[hbm] * 4,
+        out_specs=(pl.BlockSpec(memory_space=pltpu.HBM),) * 4,
+        scratch_shapes=[
+            pltpu.VMEM((n_shard, rank, cols), f32),
+            pltpu.VMEM((8, rank), f32),
+            pltpu.VMEM((n_shard, own, cols), f32),
+            pltpu.VMEM((own, width), f32),
+            pltpu.VMEM((own, width), f32),
+            pltpu.VMEM((rank, width), f32),
+            dma(3, n_chip), dma(), dma(3),
+        ],
+        compiler_params=pltpu.CompilerParams(vmem_limit_bytes=FINISH_LIMIT),
+        name="outputs",
+    )(q3, p_own, rows, dh)
     return update, error[None], q_t.T, dh_t.T
 
 

time: 57.8 us -> 50.2 us (0.87)
  local copies, waits for them, and re-layouts: 6.24 us -> 0 us
  Pallas kernels: 50.5 us -> 49.4 us
    unnamed x4 -> x0, local copies, waits for them, and re-layouts: 6.24 us -> none
    pallas_call x1, Pallas kernels: 50.5 us -> 46.6 us  [body(): pl.pallas_call(functools.partial(kernel, n_rep, n_shard, POWER, scale), o...]
    pallas_call x0 -> x1, Pallas kernels: none -> 2.84 us  [body(): pl.pallas_call(functools.partial(finish, n_rep, n_shard), out_shape=(jax....]
where the time goes in v2:
time: 50.2 us; the launch traced here: 50 us
  Pallas kernels  49.4 us (98%)
  between operations  0.64 us (1%)
    pallas_call x1, Pallas kernels, body(): pl.pallas_call(functools.partial(kernel, n_rep, n_shard, POWER, scale), o...  46.6 us
    pallas_call x1, Pallas kernels, body(): pl.pallas_call(functools.partial(finish, n_rep, n_shard), out_shape=(jax....  2.84 us

profile of v2, /device:TPU:9, one launch (start us, length us, event | category | flops | bytes accessed | tf_op | source)
XLA Modules:
  0.0 50.0 jit_solution(9891396499746725751)
XLA Ops:
  0.6 46.6 %bucket_step.1 = (f32[16,32,256]{2,1,0:T(8,128)}, f32[8,32]{1,0:T(8,128)}, f32[16,4,256]{2,1,0:T(4,128)}, bf16[64,384]{1,0:T(8,128)(2,1)}) custom-call(bf16[64,384]{1,0:T(8,128)(2,1)} %bitcast.8, bf16[384,4096]{1,0:T(8,128)(2,1)} %g_hbm.1, bf16[4,4096]{1,0:T(4,128)(2,1)} %w_hbm.1, f32[4,4096]{1,0:T(4,128)} %bitcast.7, f32[32,4096]{1,0:T(8,128)} %bitcast.6), custom_call_target="tpu_custom_call" | custom-call | tf_op jit(solution)/shard_map/bucket_step/pallas_call | solution.py:343
  47.2 2.8 %outputs.1 = (f32[4,4096]{1,0:T(4,128)}, f32[4,4096]{1,0:T(4,128)}, f32[32,4096]{1,0:T(8,128)}, bf16[64,384]{1,0:T(8,128)(2,1)}) custom-call(f32[16,32,256]{2,1,0:T(8,128)} %get-tuple-element.12.q_in, f32[8,32]{1,0:T(8,128)} %get-tuple-element.13.p_in, f32[16,4,256]{2,1,0:T(4,128)} %get-tuple-element.14.row_in, bf16[64,384]{1,0:T(8,128)(2,1)} %get-tuple-element.15.dh_in), custom_call_target="tpu_custom_call" | custom-call | tf_op jit(solution)/shard_map/outputs/pallas_call | solution.py:385
